TPU v7x, 32 devices: a whole 2x2x4 slice. The times are simulated.
32 devices in a mesh: dp: 8 (over z, core), row: 2 (over y), col: 2 (over x).
Axes of the slice: x: 2, y: 2, z: 4, core: 2. Of those that a mesh axis runs over, the one named last changes fastest.
Arguments:
- patches: bfloat16 [4096, 1408], P(('dp', 'row', 'col')), may hold values from -6 to 6
- norm_gain: float32 [1408], replicated, may hold values from 0.5 to 1.5
- norm_bias: float32 [1408], replicated, may hold values from -3 to 3
- up_weight: bfloat16 [1408, 6144], P('col', 'row'), may hold values from -0.15625 to 0.15625
- up_bias: float32 [6144], P('row'), may hold values from -3 to 3
- down_weight: bfloat16 [6144, 1408], P('row', 'col'), may hold values from -0.078125 to 0.078125
- down_bias: float32 [1408], replicated, may hold values from -3 to 3
- cotangent: bfloat16 [4096, 1408], P(('dp', 'row', 'col')), may hold values from -6 to 6
Outputs:
- output: float32 [4096, 1408], P(('dp', 'row', 'col'))
- patch_grad: float32 [4096, 1408], P(('dp', 'row', 'col'))
- up_grad: float32 [1408, 6144], P('col', 'row')
- down_grad: float32 [6144, 1408], P('row', 'col')
- bias_grad: float32 [6144], P('row')
- norm_grad: float32 [2, 1408], replicated
All inputs are finite; a program needn't handle non-finite values.
Results may differ from a plain program's by a relative error of at most 0.0055.
Values may be sent and summed in bfloat16 or wider, within the bound.
A program may use at most 128 MiB of HBM per device.

v0:
```python
import math
import jax
import jax.numpy as jnp
from jax import lax
from jax.sharding import PartitionSpec as P

EPSILON = 1e-06
GELU_ROOT = 0.7978845608028654
GELU_CUBIC = 0.044715


def gelu_value(value):
    inner = jnp.tanh(GELU_ROOT * (value + GELU_CUBIC * value * value * value))
    return 0.5 * value * (1.0 + inner)


def gelu_slope(value):
    inner = jnp.tanh(GELU_ROOT * (value + GELU_CUBIC * value * value * value))
    return 0.5 * (1.0 + inner) + 0.5 * value * (1.0 - inner * inner) * GELU_ROOT * (
        1.0 + 3.0 * GELU_CUBIC * value * value
    )


def contract_rows(left, right):
    return lax.dot_general(
        left, right, (((0,), (0,)), ((), ())), preferred_element_type=jnp.float32
    )


def contract_cols(left, right):
    return lax.dot_general(
        left, right, (((1,), (1,)), ((), ())), preferred_element_type=jnp.float32
    )


def on_device(patches, norm_gain, norm_bias, up_weight, up_bias, down_weight, down_bias, cotangent):
    n_row = lax.axis_size("row")
    n_col = lax.axis_size("col")
    n_replica = lax.axis_size("dp")
    local_rows = patches.shape[0]
    width = patches.shape[1]
    half_width = width // n_col
    group_rows = n_row * local_rows
    scaling = 1.0 / math.sqrt(local_rows * n_row * n_col * n_replica)
    wide_patches = patches.astype(jnp.float32)
    centred = wide_patches - jnp.mean(wide_patches, axis=1, keepdims=True)
    inverse_spread = lax.rsqrt(jnp.mean(centred * centred, axis=1, keepdims=True) + EPSILON)
    standard = centred * inverse_spread
    normed = (standard * norm_gain + norm_bias).astype(jnp.bfloat16)
    swapped = lax.all_to_all(normed, "col", split_axis=1, concat_axis=0, tiled=True)
    swapped = swapped.reshape(n_col, local_rows, half_width)
    gathered = lax.all_gather(swapped, "row", axis=1, tiled=True)
    normed_all = gathered.reshape(n_col * group_rows, half_width)
    preact = (
        lax.psum_scatter(
            jnp.dot(normed_all, up_weight, preferred_element_type=jnp.float32),
            "col",
            scatter_dimension=0,
            tiled=True,
        )
        + up_bias
    )
    activated = gelu_value(preact).astype(jnp.bfloat16)
    down_full = lax.all_gather(down_weight, "col", axis=1, tiled=True)
    projected = lax.psum_scatter(
        jnp.dot(activated, down_full, preferred_element_type=jnp.float32),
        "row",
        scatter_dimension=0,
        tiled=True,
    )
    output = projected + down_bias + wide_patches
    upstream = lax.all_gather(cotangent, "row", axis=0, tiled=True)
    down_partial = contract_rows(activated, upstream)
    down_grad = lax.psum_scatter(down_partial, "col", scatter_dimension=1, tiled=True)
    slope = (contract_cols(upstream, down_full) * gelu_slope(preact)).astype(jnp.bfloat16)
    slope_all = lax.all_gather(slope, "col", axis=0, tiled=True)
    up_grad = contract_rows(normed_all, slope_all)
    bias_grad = jnp.sum(slope_all.astype(jnp.float32), axis=0)
    up_grad, bias_grad, down_grad = lax.psum((up_grad, bias_grad, down_grad), "dp")
    partial_back = contract_cols(slope_all, up_weight).reshape(n_col, n_row, local_rows, half_width)
    summed_back = lax.psum_scatter(partial_back, "row", scatter_dimension=1, tiled=True)
    summed_back = summed_back.reshape(n_col, local_rows, half_width)
    normed_back = lax.all_to_all(summed_back, "col", split_axis=0, concat_axis=2, tiled=True)
    normed_back = normed_back.reshape(local_rows, width)
    norm_terms = jnp.stack([jnp.sum(normed_back * standard, axis=0), jnp.sum(normed_back, axis=0)])
    norm_grad = lax.psum(norm_terms, ("dp", "row", "col"))
    scaled = normed_back * norm_gain
    back = inverse_spread * (
        scaled
        - jnp.mean(scaled, axis=1, keepdims=True)
        - standard * jnp.mean(scaled * standard, axis=1, keepdims=True)
    )
    patch_grad = back + cotangent.astype(jnp.float32)
    return (
        output,
        patch_grad,
        up_grad * scaling,
        down_grad * scaling,
        bias_grad * scaling,
        norm_grad * scaling,
    )


def solution(mesh):
    in_specs = (
        P(("dp", "row", "col"), None),
        P(),
        P(),
        P("col", "row"),
        P("row"),
        P("row", "col"),
        P(),
        P(("dp", "row", "col"), None),
    )
    out_specs = (
        P(("dp", "row", "col"), None),
        P(("dp", "row", "col"), None),
        P("col", "row"),
        P("row", "col"),
        P("row"),
        P(),
    )
    return jax.shard_map(
        on_device, mesh=mesh, in_specs=in_specs, out_specs=out_specs, check_vma=False
    )
```

profile of v0, /device:TPU:0, one launch (start us, length us, event | category | flops | bytes accessed | tf_op | source)
XLA Modules:
  0.0 874.7 jit_solution(3099713600413117997)
XLA Ops:
  9.1 10.3 %all_to_all.31 = bf16[128,2,704]{0,2,1:T(8,128)(2,1)S(1)} all-to-all(bf16[128,2,704]{0,2,1:T(8,128)(2,1)S(1)} %bitcast.30), channel_id=1, replica_groups=mesh['dp'=8,'row'=2,'col'=2] {'col'}, dimensions={1} | all-to-all | bytes 720896 | tf_op jit(solution)/shard_map/all_to_all | solution.py:50
  19.3 9.7 %all_gather.12 = bf16[2,256,704]{1,2,0:T(8,128)(2,1)S(1)} all-gather(bf16[2,128,704]{1,2,0:T(8,128)(2,1)S(1)} %bitcast.31), channel_id=1, replica_groups=mesh['dp'=8,'row'=2,'col'=2] {'row'}, dimensions={1}, use_global_device_ids=true | all-gather | bytes 1081344 | tf_op jit(solution)/shard_map/all_gather | solution.py:52
  30.0 7.2 fusion.23
  38.2 9.0 %all_gather.14 = bf16[256,1408]{1,0:T(8,128)(2,1)} all-gather(bf16[128,1408]{1,0:T(8,128)(2,1)S(1)} %copy-done.5), channel_id=1, replica_groups=mesh['dp'=8,'row'=2,'col'=2] {'row'}, dimensions={0}, use_global_device_ids=true | all-gather | bytes 1081344 | tf_op jit(solution)/shard_map/all_gather | solution.py:72
  47.1 74.6 %all-gather.3.cloned.1.call-done = bf16[3072,1408]{0,1:T(8,128)(2,1)} async-done(((bf16[3072,704]{0,1:T(8,128)(2,1)}), bf16[3072,1408]{0,1:T(8,128)(2,1)}) %all-gather.3.cloned.1.call-update) | async-done | bytes 8650768 | tf_op jit(solution)/shard_map/all_gather | solution.py:64
  121.7 80.0 %reduce-scatter.5.cloned.1.call-done = f32[256,3072]{1,0:T(8,128)} async-done(((f32[512,3072]{1,0:T(8,128)}), f32[256,3072]{1,0:T(8,128)}) %reduce-scatter.5.cloned.1.call-update) | async-done | bytes 3145744 | tf_op jit(solution)/shard_map/reduce_scatter | solution.py:55
  201.7 9.9 %fusion = bf16[256,3072]{1,0:T(8,128)(2,1)} fusion(bf16[256,1408]{1,0:T(8,128)(2,1)} %all_gather.14, bf16[3072,1408]{0,1:T(8,128)(2,1)} %all-gather.3.cloned.1.call-done, f32[256,3072]{1,0:T(8,128)} %reduce-scatter.5.cloned.1.call-done, f32[3072]{0:T(1024)S(1)} %copy-done.8), kind=kOutput, calls=%fused_computation.6 | convolution fusion | flops 2230321152 | bytes 14102528 | tf_op jit(solution)/shard_map/dot_general | solution.py:31
  211.7 10.9 %fusion.21 = f32[3072,1408]{0,1:T(8,128)} fusion(bf16[256,1408]{1,0:T(8,128)(2,1)} %all_gather.14, f32[256,3072]{1,0:T(8,128)S(1)} %copy-done.2, f32[3072]{0:T(1024)S(1)} %copy-done.8), kind=kOutput, calls=%fused_computation.40 | convolution fusion | flops 2222456832 | bytes 21180416 | tf_op jit(solution)/shard_map/dot_general | solution.py:25
  222.9 33.8 %all-gather.5.cloned.1.call-done = bf16[512,3072]{1,0:T(8,128)(2,1)} async-done(((bf16[256,3072]{1,0:T(8,128)(2,1)}), bf16[512,3072]{1,0:T(8,128)(2,1)}) %all-gather.5.cloned.1.call-update) | async-done | bytes 3145744 | tf_op jit(solution)/shard_map/all_gather | solution.py:76
  256.7 5.6 fusion.24
  262.3 0.9 reshape.62
  263.3 1.2 copy.17
  264.6 9.0 %fusion.22 = f32[256,1408]{1,0:T(8,128)} fusion(bf16[3072,1408]{0,1:T(8,128)(2,1)} %all-gather.3.cloned.1.call-done, f32[256,3072]{1,0:T(8,128)} %reduce-scatter.5.cloned.1.call-done, f32[3072]{0:T(1024)S(1)} %copy-done.8), kind=kOutput, calls=%fused_computation.41 | convolution fusion | flops 2222456832 | bytes 13250560 | tf_op jit(solution)/shard_map/dot_general | solution.py:66
  273.6 8.0 fusion.25
  281.7 172.1 %reduce-scatter.11.cloned.1.call-done = f32[3072,704]{0,1:T(8,128)} async-done(((f32[3072,1408]{0,1:T(8,128)}), f32[3072,704]{0,1:T(8,128)}) %reduce-scatter.11.cloned.1.call-update) | async-done | bytes 8650768 | tf_op jit(solution)/shard_map/reduce_scatter | solution.py:74
  453.9 27.3 %reduce-scatter.9.cloned.1.call-done = f32[2,1,128,704]{2,3,0,1:T(8,128)} async-done(((f32[2,2,128,704]{2,3,0,1:T(8,128)}), f32[2,1,128,704]{2,3,0,1:T(8,128)}) %reduce-scatter.9.cloned.1.call-update) | async-done | bytes 720912 | tf_op jit(solution)/shard_map/reduce_scatter | solution.py:81
  481.2 3.5 all-to-all-start.1
  484.7 2.6 convert_reduce_fusion
  487.3 28.4 %psum.30 = f32[3072]{0:T(1024)S(1)} all-reduce(f32[3072]{0:T(1024)S(1)} %convert_reduce_fusion), channel_id=1, replica_groups=mesh['dp'=8,'row'=2,'col'=2] {'dp'}, use_global_device_ids=true, to_apply=%region_11.0 | all-reduce | flops 3072 | bytes 24576 | tf_op jit(solution)/shard_map/psum | solution.py:79
  517.5 38.8 %psum.31 = f32[2,1408]{1,0:T(2,128)S(1)} all-reduce(f32[2,1408]{1,0:T(2,128)S(1)} %pad_maximum_fusion), channel_id=1, replica_groups=mesh['dp'=8,'row'=2,'col'=2] {'dp','row','col'}, use_global_device_ids=true, to_apply=%region_14.0 | all-reduce | flops 2816 | bytes 22528 | tf_op jit(solution)/shard_map/psum | solution.py:86
  556.9 2.5 fusion.17
  559.4 295.5 %all-reduce.3.cloned.1.call-done = (f32[704,3072]{1,0:T(8,128)}, f32[3072,704]{0,1:T(8,128)}) async-done(((f32[704,3072]{1,0:T(8,128)}, f32[3072,704]{0,1:T(8,128)}), (f32[704,3072]{1,0:T(8,128)}, f32[3072,704]{0,1:T(8,128)})) %all-reduce.3.cloned.1.call-update) | async-done | bytes 17301520 | tf_op jit(solution)/shard_map/psum | solution.py:79
  855.0 8.6 broadcast_multiply_fusion.1
  863.5 4.3 broadcast_multiply_fusion
  (55 shorter events, 6.7 us)
Async XLA Ops:
  7.2 1.0 copy-start
  7.2 1.4 copy-start.7
  7.2 1.4 copy-start.9
  7.2 114.5 %all-gather.3.cloned.1.call-start = ((), (), s32[]{:S(2)}) async-start(), calls=%async_computation.7 | async-start | bytes 12976128 | tf_op jit(solution)/shard_map/all_gather | solution.py:64
  7.9 193.8 %reduce-scatter.5.cloned.1.call-start = ((), (), s32[]{:S(2)}) async-start(), calls=%async_computation.6 | async-start | bytes 9437184 | tf_op jit(solution)/shard_map/reduce_scatter | solution.py:55
  29.1 0.9 copy-start.3
  37.2 1.0 copy-start.5
  37.2 164.5 %copy-start.8 = (f32[3072]{0:T(1024)S(1)}, f32[3072]{0:T(1024)}, u32[]{:S(2)}) copy-start(f32[3072]{0:T(1024)} %param.12) | copy-start | bytes 36868
  37.2 219.5 %all-gather.5.cloned.1.call-start = ((), (), s32[]{:S(2)}) async-start(), calls=%async_computation.9 | async-start | bytes 4718592 | tf_op jit(solution)/shard_map/all_gather | solution.py:76
  201.7 10.0 %copy-start.2 = (f32[256,3072]{1,0:T(8,128)S(1)}, f32[256,3072]{1,0:T(8,128)}, u32[]{:S(2)}) copy-start(f32[256,3072]{1,0:T(8,128)} %reduce-scatter.5.cloned.1.call-done) | copy-start | bytes 9437188
  211.7 242.1 %reduce-scatter.11.cloned.1.call-start = ((), (), s32[]{:S(2)}) async-start(), calls=%async_computation.11 | async-start | bytes 25952256 | tf_op jit(solution)/shard_map/reduce_scatter | solution.py:74
  222.7 258.5 %reduce-scatter.9.cloned.1.call-start = ((), (), s32[]{:S(2)}) async-start(), calls=%async_computation.10 | async-start | bytes 2162688 | tf_op jit(solution)/shard_map/reduce_scatter | solution.py:81
  264.5 9.1 %copy-start.4 = (bf16[2,88,8,256]{3,2,0,1:T(8,128)(2,1)S(1)}, bf16[2,88,8,256]{3,2,0,1:T(8,128)(2,1)}, u32[]{:S(2)}) copy-start(bf16[2,88,8,256]{3,2,0,1:T(8,128)(2,1)} %copy-done.3) | copy-start | bytes 2162692
  264.5 292.4 %reduce-scatter.7.cloned.1.call-start = ((), (), s32[]{:S(2)}) async-start(), calls=%async_computation.8 | async-start | bytes 2162688 | tf_op jit(solution)/shard_map/reduce_scatter | solution.py:65
  273.6 581.4 %all-reduce.3.cloned.1.call-start = ((), (), s32[]{:S(2)}) async-start(), calls=%async_computation.12 | async-start | bytes 34603008 | tf_op jit(solution)/shard_map/psum | solution.py:79
  481.2 35.1 %all-to-all-start.1 = ((f32[2,128,704]{1,2,0:T(8,128)}), f32[2,128,704]{1,2,0:T(8,128)S(1)}, u32[]{:S(2)}, u32[]{:S(2)}) async-start(f32[2,128,704]{1,2,0:T(8,128)} %bitcast.32), calls=%async_computation.4 | async-start | bytes 1441792 | tf_op jit(solution)/shard_map/all_to_all | solution.py:83
  484.7 72.2 %copy-start.6 = (bf16[128,1408]{1,0:T(8,128)(2,1)S(1)}, bf16[128,1408]{1,0:T(8,128)(2,1)}, u32[]{:S(2)}) copy-start(bf16[128,1408]{1,0:T(8,128)(2,1)} %param.15) | copy-start | bytes 1081348
  484.7 72.2 %copy-start.10 = (f32[1408]{0:T(1024)S(1)}, f32[1408]{0:T(1024)}, u32[]{:S(2)}) copy-start(f32[1408]{0:T(1024)} %param.14) | copy-start | bytes 16900
  855.0 8.6 copy-start.1
Sparse Core Ops, SparseCore 0:
  9.6 112.0 all-gather.2
  124.5 77.1 reduce-scatter.4
  211.8 44.8 all-gather.4
  258.9 194.8 reduce-scatter.10
  456.4 24.6 reduce-scatter.8
  483.3 24.6 reduce-scatter.6
  511.2 343.7 all-reduce.2
where the time goes:
time: 875 us
  waiting for transfers between devices  684 us (78%)
  blocking collectives  96.1 us (11%)
  matrix products  50.6 us (6%)
  other arithmetic  20.7 us (2%)
  between operations  14.3 us (2%)
    psum x1, waiting for transfers between devices, on_device(): lax.psum((up_grad, bias_grad, down_grad), 'dp')  296 us
    reduce_scatter x1, waiting for transfers between devices, on_device(): lax.psum_scatter(down_partial, 'col', scatter_dimension=1, tiled=True)  172 us
    reduce_scatter x1, waiting for transfers between devices, on_device(): lax.psum_scatter(jnp.dot(normed_all, up_weight, preferred_element_type=jn...  80 us
    all_gather x1, waiting for transfers between devices, on_device(): down_full = lax.all_gather(down_weight, 'col', axis=1, tiled=True)  74.6 us
    psum x1, blocking collectives, on_device(): norm_grad = lax.psum(norm_terms, ('dp', 'row', 'col'))  38.8 us
    all_gather x1, waiting for transfers between devices, on_device(): slope_all = lax.all_gather(slope, 'col', axis=0, tiled=True)  33.8 us
    psum x1, blocking collectives, on_device(): lax.psum((up_grad, bias_grad, down_grad), 'dp')  28.4 us
    reduce_scatter x1, waiting for transfers between devices, on_device(): lax.psum_scatter(partial_back, 'row', scatter_dimension=1, tiled=True)  27.3 us
  transfers between devices with their start and end apart: 8, of which 6 were waited for; matrix products, arithmetic and copies ran while one was open for 6% of the time, Pallas kernels for 0%

commit v1 on v0

--- a/solution.py
+++ b/solution.py
@@ -61,7 +61,11 @@
         + up_bias
     )
     activated = gelu_value(preact).astype(jnp.bfloat16)
-    down_full = lax.all_gather(down_weight, "col", axis=1, tiled=True)
+    down_full = jnp.roll(
+        jnp.concatenate([down_weight, lax.ppermute(down_weight, "col", [(0, 1), (1, 0)])], axis=1),
+        lax.axis_index("col") * down_weight.shape[1],
+        axis=1,
+    )
     projected = lax.psum_scatter(
         jnp.dot(activated, down_full, preferred_element_type=jnp.float32),
         "row",

time: 875 us -> 892 us (1.019)
  other arithmetic: 20.7 us -> 41.4 us
    ppermute x0 -> x1, waiting for transfers between devices: none -> 151 us  [on_device(): lax.ppermute(down_weight, 'col', [(0, 1), (1, 0)])]
    reduce_scatter x1, waiting for transfers between devices: 80 us -> 0.01 us  [on_device(): lax.psum_scatter(jnp.dot(normed_all, up_weight, preferred_element_type=jn...]
    all_gather x1 -> x0, waiting for transfers between devices: 74.6 us -> none  [on_device(): down_full = lax.all_gather(down_weight, 'col', axis=1, tiled=True)]
    concatenate x0 -> x1, other arithmetic: none -> 17.8 us  [on_device(): jnp.roll(jnp.concatenate([down_weight, lax.ppermute(down_weight, 'col', [...]
  transfers between devices with their start and end apart: 8 -> 8, of which waited for: 6 -> 5; matrix products, arithmetic and copies ran while one was open for 6% -> 7% of each run, Pallas kernels for 0% -> 0%
where the time goes in v1:
time: 892 us; the launch traced here: 891 us
  waiting for transfers between devices  681 us (76%)
  blocking collectives  95.9 us (11%)
  matrix products  50 us (6%)
  other arithmetic  41.4 us (5%)
  between operations  14.2 us (2%)
    psum x1, waiting for transfers between devices, on_device(): lax.psum((up_grad, bias_grad, down_grad), 'dp')  296 us
    reduce_scatter x1, waiting for transfers between devices, on_device(): lax.psum_scatter(down_partial, 'col', scatter_dimension=1, tiled=True)  172 us
    ppermute x1, waiting for transfers between devices, on_device(): lax.ppermute(down_weight, 'col', [(0, 1), (1, 0)])  151 us
    psum x1, blocking collectives, on_device(): norm_grad = lax.psum(norm_terms, ('dp', 'row', 'col'))  38.6 us
    all_gather x1, waiting for transfers between devices, on_device(): slope_all = lax.all_gather(slope, 'col', axis=0, tiled=True)  34.9 us
    psum x1, blocking collectives, on_device(): lax.psum((up_grad, bias_grad, down_grad), 'dp')  28.4 us
    reduce_scatter x1, waiting for transfers between devices, on_device(): lax.psum_scatter(partial_back, 'row', scatter_dimension=1, tiled=True)  26.6 us
    dot_general x2, matrix products, contract_rows(): lax.dot_general(left, right, (((0,), (0,)), ((), ())), preferred_element_...  18.7 us
  transfers between devices with their start and end apart: 8, of which 5 were waited for; matrix products, arithmetic and copies ran while one was open for 7% of the time, Pallas kernels for 0%

profile of v1, /device:TPU:0, one launch (start us, length us, event | category | flops | bytes accessed | tf_op | source)
XLA Modules:
  0.0 891.4 jit_solution(7184788667319267889)
XLA Ops:
  8.3 1.2 fusion.23
  9.6 1.3 fusion.17
  11.1 10.3 %all_to_all.31 = bf16[128,2,704]{0,2,1:T(8,128)(2,1)S(1)} all-to-all(bf16[128,2,704]{0,2,1:T(8,128)(2,1)S(1)} %bitcast.36), channel_id=1, replica_groups=mesh['dp'=8,'row'=2,'col'=2] {'col'}, dimensions={1} | all-to-all | bytes 720896 | tf_op jit(solution)/shard_map/all_to_all | solution.py:50
  21.4 9.7 %all_gather.9 = bf16[2,256,704]{1,2,0:T(8,128)(2,1)S(1)} all-gather(bf16[2,128,704]{1,2,0:T(8,128)(2,1)S(1)} %bitcast.37), channel_id=1, replica_groups=mesh['dp'=8,'row'=2,'col'=2] {'row'}, dimensions={1}, use_global_device_ids=true | all-gather | bytes 1081344 | tf_op jit(solution)/shard_map/all_gather | solution.py:52
  32.0 6.8 fusion.27
  39.7 8.9 %all_gather.10 = bf16[256,1408]{1,0:T(8,128)(2,1)} all-gather(bf16[128,1408]{1,0:T(8,128)(2,1)S(1)} %copy-done.5), channel_id=1, replica_groups=mesh['dp'=8,'row'=2,'col'=2] {'row'}, dimensions={0}, use_global_device_ids=true | all-gather | bytes 1081344 | tf_op jit(solution)/shard_map/all_gather | solution.py:76
  48.7 151.1 %collective-permute-done = bf16[3072,704]{0,1:T(8,128)(2,1)} collective-permute-done((bf16[3072,704]{0,1:T(8,128)(2,1)}, bf16[3072,704]{0,1:T(8,128)(2,1)}, u32[]{:S(2)}, u32[]{:S(2)}) %collective-permute-start) | collective-permute-done | bytes 4325408 | tf_op jit(solution)/shard_map/ppermute | solution.py:65
  199.8 17.8 %fusion.2 = bf16[3072,1408]{0,1:T(8,128)(2,1)} fusion(s32[]{:T(128)S(6)} %select_n.14, bf16[3072,704]{0,1:T(8,128)(2,1)} %param.13, bf16[3072,704]{0,1:T(8,128)(2,1)} %collective-permute-done), kind=kLoop, calls=%fused_computation.6 | loop fusion | flops 34603008 | bytes 17301508 | tf_op jit(solution)/shard_map/jit(_roll_dynamic)/concatenate | solution.py:64
  217.6 9.9 %fusion.4 = bf16[256,3072]{1,0:T(8,128)(2,1)} fusion(bf16[256,1408]{1,0:T(8,128)(2,1)} %all_gather.10, bf16[3072,1408]{0,1:T(8,128)(2,1)} %fusion.2, f32[256,3072]{1,0:T(8,128)} %reduce-scatter.5.cloned.1.call-done, f32[3072]{0:T(1024)S(1)} %copy-done.7), kind=kOutput, calls=%fused_computation.14 | convolution fusion | flops 2230321152 | bytes 14102528 | tf_op jit(solution)/shard_map/dot_general | solution.py:31
  227.7 10.7 %fusion.25 = f32[3072,1408]{0,1:T(8,128)} fusion(bf16[256,1408]{1,0:T(8,128)(2,1)} %all_gather.10, f32[256,3072]{1,0:T(8,128)S(1)} %copy-done.2, f32[3072]{0:T(1024)S(1)} %copy-done.7), kind=kOutput, calls=%fused_computation.48 | convolution fusion | flops 2222456832 | bytes 21180416 | tf_op jit(solution)/shard_map/dot_general | solution.py:25
  238.5 34.9 %all-gather.2.cloned.1.call-done = bf16[512,3072]{1,0:T(8,128)(2,1)} async-done(((bf16[256,3072]{1,0:T(8,128)(2,1)}), bf16[512,3072]{1,0:T(8,128)(2,1)}) %all-gather.2.cloned.1.call-update) | async-done | bytes 3145744 | tf_op jit(solution)/shard_map/all_gather | solution.py:80
  273.4 5.6 fusion.28
  281.3 9.0 %fusion.26 = f32[256,1408]{1,0:T(8,128)} fusion(bf16[3072,1408]{0,1:T(8,128)(2,1)} %fusion.2, f32[256,3072]{1,0:T(8,128)} %reduce-scatter.5.cloned.1.call-done, f32[3072]{0:T(1024)S(1)} %copy-done.7), kind=kOutput, calls=%fused_computation.49 | convolution fusion | flops 2222456832 | bytes 13250560 | tf_op jit(solution)/shard_map/dot_general | solution.py:70
  290.3 8.0 fusion.29
  298.4 172.2 %reduce-scatter.11.cloned.1.call-done = f32[3072,704]{0,1:T(8,128)} async-done(((f32[3072,1408]{0,1:T(8,128)}), f32[3072,704]{0,1:T(8,128)}) %reduce-scatter.11.cloned.1.call-update) | async-done | bytes 8650768 | tf_op jit(solution)/shard_map/reduce_scatter | solution.py:78
  471.4 26.6 %reduce-scatter.9.cloned.1.call-done = f32[2,1,128,704]{2,3,0,1:T(8,128)} async-done(((f32[2,2,128,704]{2,3,0,1:T(8,128)}), f32[2,1,128,704]{2,3,0,1:T(8,128)}) %reduce-scatter.9.cloned.1.call-update) | async-done | bytes 720912 | tf_op jit(solution)/shard_map/reduce_scatter | solution.py:85
  498.0 3.7 all-to-all-start.1
  501.7 2.5 convert_reduce_fusion
  504.2 28.4 %psum.30 = f32[3072]{0:T(1024)S(1)} all-reduce(f32[3072]{0:T(1024)S(1)} %convert_reduce_fusion), channel_id=1, replica_groups=mesh['dp'=8,'row'=2,'col'=2] {'dp'}, use_global_device_ids=true, to_apply=%region_11.12 | all-reduce | flops 3072 | bytes 24576 | tf_op jit(solution)/shard_map/psum | solution.py:83
  534.4 38.6 %psum.31 = f32[2,1408]{1,0:T(2,128)S(1)} all-reduce(f32[2,1408]{1,0:T(2,128)S(1)} %pad_maximum_fusion), channel_id=1, replica_groups=mesh['dp'=8,'row'=2,'col'=2] {'dp','row','col'}, use_global_device_ids=true, to_apply=%region_14.15 | all-reduce | flops 2816 | bytes 22528 | tf_op jit(solution)/shard_map/psum | solution.py:90
  573.6 2.5 fusion.21
  576.1 295.5 %all-reduce.3.cloned.1.call-done = (f32[704,3072]{1,0:T(8,128)}, f32[3072,704]{0,1:T(8,128)}) async-done(((f32[704,3072]{1,0:T(8,128)}, f32[3072,704]{0,1:T(8,128)}), (f32[704,3072]{1,0:T(8,128)}, f32[3072,704]{0,1:T(8,128)})) %all-reduce.3.cloned.1.call-update) | async-done | bytes 17301520 | tf_op jit(solution)/shard_map/psum | solution.py:83
  871.7 8.6 broadcast_multiply_fusion.1
  880.2 4.3 broadcast_multiply_fusion
  (51 shorter events, 9.0 us)
Async XLA Ops:
  7.2 210.4 %reduce-scatter.5.cloned.1.call-start = ((), (), s32[]{:S(2)}) async-start(), calls=%async_computation.6 | async-start | bytes 9437184 | tf_op jit(solution)/shard_map/reduce_scatter | solution.py:55
  31.1 0.9 copy-start.3
  38.8 1.0 copy-start.5
  38.8 234.6 %all-gather.2.cloned.1.call-start = ((), (), s32[]{:S(2)}) async-start(), calls=%async_computation.8 | async-start | bytes 4718592 | tf_op jit(solution)/shard_map/all_gather | solution.py:80
  38.8 160.9 %collective-permute-start = (bf16[3072,704]{0,1:T(8,128)(2,1)}, bf16[3072,704]{0,1:T(8,128)(2,1)}, u32[]{:S(2)}, u32[]{:S(2)}) collective-permute-start(bf16[3072,704]{0,1:T(8,128)(2,1)} %param.13), channel_id=1, source_target_pairs={{0,1},{1,0},{2,3},{3,2},{4,5},{5,4},{6,7},{7,6},{8,9},{9,8},{10,11... | collective-permute-start | bytes 12976136 | tf_op jit(solution)/shard_map/ppermute | solution.py:65
  48.7 168.8 %copy-start.7 = (f32[3072]{0:T(1024)S(1)}, f32[3072]{0:T(1024)}, u32[]{:S(2)}) copy-start(f32[3072]{0:T(1024)} %param.12) | copy-start | bytes 36868
  217.5 10.2 %copy-start.2 = (f32[256,3072]{1,0:T(8,128)S(1)}, f32[256,3072]{1,0:T(8,128)}, u32[]{:S(2)}) copy-start(f32[256,3072]{1,0:T(8,128)} %reduce-scatter.5.cloned.1.call-done) | copy-start | bytes 9437188
  227.5 243.1 %reduce-scatter.11.cloned.1.call-start = ((), (), s32[]{:S(2)}) async-start(), calls=%async_computation.10 | async-start | bytes 25952256 | tf_op jit(solution)/shard_map/reduce_scatter | solution.py:78
  238.5 259.6 %reduce-scatter.9.cloned.1.call-start = ((), (), s32[]{:S(2)}) async-start(), calls=%async_computation.9 | async-start | bytes 2162688 | tf_op jit(solution)/shard_map/reduce_scatter | solution.py:85
  281.2 9.1 %copy-start.4 = (bf16[2,88,8,256]{3,2,0,1:T(8,128)(2,1)S(1)}, bf16[2,88,8,256]{3,2,0,1:T(8,128)(2,1)}, u32[]{:S(2)}) copy-start(bf16[2,88,8,256]{3,2,0,1:T(8,128)(2,1)} %copy-done.3) | copy-start | bytes 2162692
  281.2 292.4 %reduce-scatter.7.cloned.1.call-start = ((), (), s32[]{:S(2)}) async-start(), calls=%async_computation.7 | async-start | bytes 2162688 | tf_op jit(solution)/shard_map/reduce_scatter | solution.py:69
  290.3 581.4 %all-reduce.3.cloned.1.call-start = ((), (), s32[]{:S(2)}) async-start(), calls=%async_computation.11 | async-start | bytes 34603008 | tf_op jit(solution)/shard_map/psum | solution.py:83
  470.6 0.7 copy-start.6
  498.0 36.0 %copy-start = (bf16[128,1408]{1,0:T(8,128)(2,1)S(1)}, bf16[128,1408]{1,0:T(8,128)(2,1)}, u32[]{:S(2)}) copy-start(bf16[128,1408]{1,0:T(8,128)(2,1)} %param.8) | copy-start | bytes 1081348
  498.0 35.2 %all-to-all-start.1 = ((f32[2,128,704]{1,2,0:T(8,128)}), f32[2,128,704]{1,2,0:T(8,128)S(1)}, u32[]{:S(2)}, u32[]{:S(2)}) async-start(f32[2,128,704]{1,2,0:T(8,128)} %bitcast.38), calls=%async_computation.4 | async-start | bytes 1441792 | tf_op jit(solution)/shard_map/all_to_all | solution.py:87
  501.7 71.9 %copy-start.8 = (f32[1408]{0:T(1024)S(1)}, f32[1408]{0:T(1024)}, u32[]{:S(2)}) copy-start(f32[1408]{0:T(1024)} %param.14) | copy-start | bytes 16900
  871.7 8.6 copy-start.1
Sparse Core Ops, SparseCore 0:
  38.9 145.1 reduce-scatter.4
  227.6 45.7 all-gather.1
  275.7 194.8 reduce-scatter.10
  473.3 24.6 reduce-scatter.8
  500.1 24.7 reduce-scatter.6
  527.9 343.6 all-reduce.2
